TPU v7x, 32 devices: a whole 2x2x4 slice. The times are simulated.
32 devices in a mesh: trans: 16 (over z, y, x), los: 2 (over core).
Axes of the slice: x: 2, y: 2, z: 4, core: 2. Of those that a mesh axis runs over, the one named last changes fastest.
Arguments:
- density: bfloat16 [2, 2048, 2048], P('los', 'trans'), may hold values from -6 to 6
- row_pos: float32 [2, 2048], replicated, may hold values from 0 to 2048
- col_pos: float32 [2, 2048], replicated, may hold values from 0 to 2048
- plane_of_slot: int32 [2], replicated, may hold values from 0 to 1, each once
- plane_bin: int32 [2], replicated, may hold values from 0 to 3, as said below
- efficiency: float32 [4, 2], replicated, may hold values from 0.3 to 3
Outputs:
- shear: float32 [2, 4, 2048, 2048], P(None, None, ('trans', 'los'))
Inputs may be any that keep to these rules, and one draw needn't show every extreme that they name: `plane_bin`: some plane has bin 0 and some plane has bin 4 - 1.
All inputs are finite; a program needn't handle non-finite values.
Results may differ from a plain program's by a relative error of at most 0.006.
Values may be sent and summed in bfloat16 or wider, within the bound.
A program may use at most 64 MiB of HBM per device.

v0:
```python
import math
import jax
import jax.numpy as jnp
from jax import lax
from jax.sharding import PartitionSpec as P


def hat_block(positions, mesh_cells):
    cells = jnp.arange(mesh_cells, dtype=jnp.int32).astype(jnp.float32)
    offset = positions[:, None] - cells[None, :] + 0.5 * mesh_cells
    folded = jnp.mod(offset, 1.0 * mesh_cells) - 0.5 * mesh_cells
    return jnp.maximum(1.0 - jnp.abs(folded), 0.0).astype(jnp.bfloat16)


def trig_pair(rows_n, cols_n, modulus, sign_value):
    product_index = (
        jnp.arange(rows_n, dtype=jnp.int32)[:, None]
        * jnp.arange(cols_n, dtype=jnp.int32)[None, :]
        % modulus
    )
    angle = product_index.astype(jnp.float32) * (2.0 * math.pi / modulus)
    return (jnp.cos(angle), sign_value * jnp.sin(angle))


def fourier(real_part, imag_part, inverse):
    length = real_part.shape[-1]
    factor_one = 16
    second = length // factor_one
    sign_value = 1.0 if inverse else -1.0
    lead_shape = real_part.shape[:-1]
    highest = lax.Precision.HIGHEST
    cos_one, sin_one = trig_pair(factor_one, factor_one, factor_one, sign_value)
    real_grid = real_part.reshape(lead_shape + (factor_one, second))
    imag_grid = imag_part.reshape(lead_shape + (factor_one, second))

    def first_pass(table, values):
        return jnp.einsum("kn,...nm->...km", table, values, precision=highest)

    section_real = first_pass(cos_one, real_grid) - first_pass(sin_one, imag_grid)
    section_imag = first_pass(cos_one, imag_grid) + first_pass(sin_one, real_grid)
    cos_twid, sin_twid = trig_pair(factor_one, second, length, sign_value)
    turned_real = section_real * cos_twid - section_imag * sin_twid
    turned_imag = section_real * sin_twid + section_imag * cos_twid
    cos_two, sin_two = trig_pair(second, second, second, sign_value)

    def second_pass(values, table):
        return jnp.einsum("...km,mj->...kj", values, table, precision=highest)

    out_real = second_pass(turned_real, cos_two) - second_pass(turned_imag, sin_two)
    out_imag = second_pass(turned_real, sin_two) + second_pass(turned_imag, cos_two)
    out_real = jnp.swapaxes(out_real, -1, -2).reshape(lead_shape + (length,))
    out_imag = jnp.swapaxes(out_imag, -1, -2).reshape(lead_shape + (length,))
    scale = 1.0 / length if inverse else 1.0
    return (out_real * scale, out_imag * scale)


def wave_numbers(index_all, length):
    return jnp.where(index_all < length // 2, index_all, index_all - length).astype(jnp.float32)


def body(density, row_pos, col_pos, plane_of_slot, plane_bin, efficiency):
    count_trans = lax.axis_size("trans")
    count_los = lax.axis_size("los")
    per_device = density.shape[0]
    mesh_cells = density.shape[2]
    grid_cells = row_pos.shape[1]
    planes_total = row_pos.shape[0]
    bins_total = efficiency.shape[0]
    width_cols = grid_cells // (count_trans * count_los)
    block_rows = min(512, grid_cells)
    slots = jnp.arange(planes_total, dtype=jnp.int32)
    bin_index = jnp.arange(bins_total, dtype=jnp.int32)
    by_columns = lax.all_to_all(density, "trans", split_axis=2, concat_axis=1, tiled=True)
    local_slot = 0
    slot_now = lax.axis_index("los") * per_device + local_slot
    plane_id = jnp.sum(jnp.where(slots == slot_now, plane_of_slot, 0))
    chosen = slots == plane_id
    plane_eff = jnp.sum(jnp.where(chosen[None, :], efficiency, 0.0), axis=1)
    first_bin = jnp.sum(jnp.where(chosen, plane_bin, 0))
    weight_list = [plane_eff * (bin_index >= first_bin).astype(jnp.float32)]
    rows_here = jnp.sum(jnp.where(chosen[:, None], row_pos, 0.0), axis=0)
    cols_here = jnp.sum(jnp.where(chosen[:, None], col_pos, 0.0), axis=0)
    pieces = []
    for begin in range(0, grid_cells, block_rows):
        row_block = hat_block(rows_here[begin : begin + block_rows], mesh_cells)
        pieces.append(
            lax.dot_general(
                by_columns[local_slot],
                row_block,
                (((0,), (1,)), ((), ())),
                preferred_element_type=jnp.float32,
            )
        )
    resampled = [jnp.concatenate(pieces, axis=1).astype(jnp.bfloat16)]
    col_tables = [hat_block(cols_here, mesh_cells)]
    half_columns = jnp.stack(resampled)
    exchanged = lax.all_to_all(half_columns, "trans", split_axis=2, concat_axis=1, tiled=True)
    local_slot = 0
    rows_map = lax.dot_general(
        exchanged[local_slot],
        col_tables[local_slot],
        (((0,), (1,)), ((), ())),
        preferred_element_type=jnp.float32,
    )
    plane_term = weight_list[local_slot][None, :, None] * rows_map[:, None, :]
    term_real, term_imag = fourier(plane_term, jnp.zeros_like(plane_term), False)
    summed_real, summed_imag = (
        lax.psum_scatter(term_real, "los", scatter_dimension=2, tiled=True),
        lax.psum_scatter(term_imag, "los", scatter_dimension=2, tiled=True),
    )
    arrived = lax.all_to_all(
        jnp.stack([summed_real, summed_imag]), "trans", split_axis=3, concat_axis=1, tiled=True
    )
    columns_local = arrived.transpose(0, 2, 3, 1)
    col_index = (
        lax.axis_index("los") * (grid_cells // count_los)
        + lax.axis_index("trans") * width_cols
        + jnp.arange(width_cols, dtype=jnp.int32)
    )
    freq_real, freq_imag = fourier(columns_local[0], columns_local[1], False)
    wave_rows = wave_numbers(jnp.arange(grid_cells, dtype=jnp.int32), grid_cells)[None, :]
    wave_cols = wave_numbers(col_index, grid_cells)[:, None]
    square_sum = jnp.maximum(wave_rows * wave_rows + wave_cols * wave_cols, 1.0)
    first_factor = (wave_rows * wave_rows - wave_cols * wave_cols) / square_sum
    second_factor = 2.0 * wave_rows * wave_cols / square_sum
    kernel_real = first_factor * freq_real - second_factor * freq_imag
    kernel_imag = first_factor * freq_imag + second_factor * freq_real
    back_real, back_imag = fourier(kernel_real, kernel_imag, True)
    returned = jnp.stack([back_real, back_imag]).transpose(0, 3, 1, 2)
    rows_local = lax.all_to_all(
        lax.all_to_all(returned, "trans", split_axis=1, concat_axis=3, tiled=True),
        "los",
        split_axis=1,
        concat_axis=3,
        tiled=True,
    )
    final_real, final_imag = fourier(rows_local[0], rows_local[1], True)
    return jnp.stack([final_real, final_imag]).transpose(0, 2, 1, 3)


def solution(mesh):
    placed = (P("los", "trans", None), P(), P(), P(), P(), P())
    return jax.shard_map(
        body,
        mesh=mesh,
        in_specs=placed,
        out_specs=P(None, None, ("trans", "los"), None),
        check_vma=False,
    )
```

profile of v0, /device:TPU:0, one launch (start us, length us, event | category | flops | bytes accessed | tf_op | source)
XLA Modules:
  0.0 628.0 jit_solution(389081637381458077)
XLA Ops:
  9.4 11.4 %reduce = bf16[2048,128]{1,0:T(8,128)(2,1)S(1)} reduce(bf16[2048,1,128]{2,1,0:T(2,128)(2,1)S(1)} %bitcast.333, bf16[]{:T(256)} %broadcast.788), dimensions={1}, to_apply=%bitcast.274.reduce_sub_computation | reduce | bytes 1048578
  21.8 8.9 %all-to-all-start = ((bf16[16,2,8192]{2,1,0:T(2,128)(2,1)}), bf16[16,2,8192]{2,1,0:T(2,128)(2,1)S(1)}, u32[]{:S(2)}, u32[]{:S(2)}) async-start(bf16[16,2,8192]{2,1,0:T(2,128)(2,1)} %reshape.416), calls=%async_computation | async-start | bytes 1048576 | tf_op jit(solution)/shard_map/all_to_all | solution.py:73
  32.2 13.6 %all-to-all-done = bf16[16,2,8192]{2,1,0:T(2,128)(2,1)S(1)} async-done(((bf16[16,2,8192]{2,1,0:T(2,128)(2,1)}), bf16[16,2,8192]{2,1,0:T(2,128)(2,1)S(1)}, u32[]{:S(2)}, u32[]{:S(2)}) %all-to-all-start) | async-done | bytes 524320 | tf_op jit(solution)/shard_map/all_to_all | solution.py:73
  46.6 3.8 fusion.108
  50.4 3.8 fusion.111
  54.2 3.8 fusion.114
  57.9 3.8 fusion.117
  61.7 8.1 %copy.182 = bf16[1,128,2048]{1,0,2:T(2,128)(2,1)S(1)} copy(bf16[1,128,2048]{1,2,0:T(8,128)(2,1)S(1)} %pad_maximum_fusion.1) | data formatting | bytes 1048576 | tf_op jit(solution)/shard_map/concatenate | solution.py:94
  69.9 11.6 %reduce.1 = bf16[2048,128]{1,0:T(8,128)(2,1)S(1)} reduce(bf16[2048,1,128]{2,1,0:T(2,128)(2,1)S(1)} %bitcast.334, bf16[]{:T(256)} %broadcast.788), dimensions={1}, to_apply=%bitcast.300.reduce_sub_computation | reduce | bytes 1048578
  82.4 4.0 all-to-all-start.1
  88.5 12.4 %all-to-all-done.1 = bf16[16,2,8192]{2,1,0:T(2,128)(2,1)S(1)} async-done(((bf16[16,2,8192]{2,1,0:T(2,128)(2,1)}), bf16[16,2,8192]{2,1,0:T(2,128)(2,1)S(1)}, u32[]{:S(2)}, u32[]{:S(2)}) %all-to-all-start.1) | async-done | bytes 524320 | tf_op jit(solution)/shard_map/all_to_all | solution.py:97
  102.0 12.7 %fusion.8 = f32[128,16,128]{2,0,1:T(8,128)S(1)} fusion(bf16[2048,128,1]{0,1,2:T(8,128)(2,1)S(1)} %reshape.400, f32[2048]{0:T(1024)S(1)} %iota_convert_fusion, f32[16,128]{1,0:T(8,128)S(1)} %bitcast.343), kind=kOutput, calls=%fused_computation.12 | convolution fusion | flops 1128267776 | bytes 1589248 | tf_op jit(solution)/shard_map/dot_general | solution.py:99
  115.4 4.1 fusion.12
  119.5 3.9 fusion.10
  125.3 3.2 fusion.36
  128.5 6.5 %fusion.52 = f32[128,4,16,128]{0,3,2,1:T(8,128)S(1)} fusion(f32[128,4,16,128]{3,2,1,0:T(8,128)S(1)} %get-tuple-element.10), kind=kOutput, calls=%fused_computation.75 | convolution fusion | flops 1610858496 | bytes 8388608 | tf_op jit(solution)/shard_map/...km,mj->...kj/dot_general | solution.py:47
  135.1 6.7 %subtract_bitcast_fusion = f32[128,4,128,16]{0,2,3,1:T(8,128)S(1)} fusion(f32[128,4,16,128]{0,3,2,1:T(8,128)S(1)} %fusion.52, f32[128,4,16,128]{3,2,1,0:T(8,128)S(1)} %get-tuple-element.9), kind=kOutput, calls=%fused_computation.56 | convolution fusion | flops 1611890688 | bytes 12582912 | tf_op jit(solution)/shard_map/...km,mj->...kj/dot_general | solution.py:47
  141.8 4.4 copy.117
  146.2 9.4 %fusion.50 = f32[128,4,16,128]{0,3,2,1:T(8,128)S(1)} fusion(f32[128,4,16,128]{3,2,1,0:T(8,128)} %copy-done.5), kind=kOutput, calls=%fused_computation.73 | convolution fusion | flops 1610842112 | bytes 8388608 | tf_op jit(solution)/shard_map/...km,mj->...kj/dot_general | solution.py:47
  155.7 6.5 %add_bitcast_fusion = f32[128,4,128,16]{0,2,3,1:T(8,128)S(1)} fusion(f32[128,4,16,128]{0,3,2,1:T(8,128)S(1)} %fusion.50, f32[128,4,16,128]{3,2,1,0:T(8,128)S(1)} %copy-done.4), kind=kOutput, calls=%fused_computation.55 | convolution fusion | flops 1611907072 | bytes 12582912 | tf_op jit(solution)/shard_map/...km,mj->...kj/dot_general | solution.py:47
  162.2 4.4 copy.122
  166.7 10.4 %reduce-scatter.5.cloned.1.call-done = f32[128,4,1024]{0,2,1:T(8,128)} async-done(((f32[128,4,2048]{0,2,1:T(8,128)}), f32[128,4,1024]{0,2,1:T(8,128)}) %reduce-scatter.5.cloned.1.call-update) | async-done | bytes 2097168 | tf_op jit(solution)/shard_map/reduce_scatter | solution.py:109
  179.7 4.9 copy.123
  184.6 7.0 %all-to-all-start.2 = ((f32[2,128,4,1024]{1,2,0,3:T(4,128)}), f32[2,128,4,1024]{1,2,0,3:T(4,128)}, u32[]{:S(2)}, u32[]{:S(2)}) async-start(f32[2,128,4,1024]{1,2,0,3:T(4,128)} %copy.123), calls=%async_computation.4 | async-start | bytes 8388608 | tf_op jit(solution)/shard_map/all_to_all | solution.py:111
  193.2 78.7 %all-to-all-done.2 = f32[2,128,4,1024]{1,2,0,3:T(4,128)} async-done(((f32[2,128,4,1024]{1,2,0,3:T(4,128)}), f32[2,128,4,1024]{1,2,0,3:T(4,128)}, u32[]{:S(2)}, u32[]{:S(2)}) %all-to-all-start.2) | async-done | bytes 4194336 | tf_op jit(solution)/shard_map/all_to_all | solution.py:111
  271.9 3.0 copy.124
  284.6 2.6 fusion.125
  287.2 3.4 fusion.123
  290.6 3.5 subtract_bitcast_fusion.1
  294.1 4.4 copy.126
  298.5 5.6 add_bitcast_fusion.1
  304.1 4.5 copy.127
  308.6 8.7 %fusion.34 = (f32[4,64,16,128]{1,3,2,0:T(8,128)}, f32[4,64,16,128]{1,3,2,0:T(8,128)}) fusion(f32[64,16,128]{0,2,1:T(8,128)S(1)} %copy-done.15, f32[64,16,128]{0,2,1:T(8,128)S(1)} %get-tuple-element.15, f32[4,64,16,128]{1,3,2,0:T(8,128)} %bitcast.325, f32[4,64,16,128]{1,3,2,0:T(8,128)} %bitcast.323), kind=kLoop, calls=%fused_computation.45 | loop fusion | flops 3145728 | bytes 9437184 | tf_op jit(solution)/shard_map/sub | solution.py:126
  317.4 3.1 copy.128
  320.4 3.3 fusion.208
  323.7 3.2 copy.129
  330.3 3.7 convolution_subtract_fusion.2
  338.1 3.4 fusion.129
  341.6 3.9 multiply_bitcast_fusion.3
  345.5 4.4 copy.132
  349.9 5.6 multiply_bitcast_fusion.2
  355.5 4.4 copy.133
  359.9 4.1 maximum_bitcast_fusion
  364.1 15.3 %copy.181 = f32[2,2048,4,64]{3,2,0,1:T(4,128)} copy(f32[2,2048,4,64]{3,1,2,0:T(8,128)S(1)} %maximum_bitcast_fusion) | data formatting | bytes 8388608 | tf_op jit(solution)/shard_map/transpose | solution.py:129
  379.4 14.6 %reshape.420 = f32[16,1,65536]{2,1,0:T(1,128)} reshape(f32[2048,2,4,64]{3,2,1,0:T(4,128)} %bitcast.312) | data formatting | bytes 8388608
  393.9 113.6 %all_to_all.81 = f32[16,1,65536]{2,1,0:T(1,128)} all-to-all(f32[16,1,65536]{2,1,0:T(1,128)} %reshape.420), channel_id=1, replica_groups=mesh['trans'=16,'los'=2] {'trans'}, dimensions={0} | all-to-all | bytes 8388608 | tf_op jit(solution)/shard_map/all_to_all | solution.py:131
  508.2 13.8 %reduce.2 = f32[16,65536]{1,0:T(8,128)} reduce(f32[16,1,65536]{2,1,0:T(1,128)} %all_to_all.81, f32[]{:T(128)} %broadcast.790), dimensions={1}, to_apply=%all_to_all.69.reduce_sub_computation | reduce | bytes 8388612 | tf_op jit(solution)/shard_map/all_to_all | solution.py:131
  522.0 9.3 %reshape.421 = f32[2048,2,4,64]{3,2,1,0:T(4,128)} reshape(f32[16,65536]{1,0:T(8,128)} %reduce.2) | data formatting | bytes 8388608
  531.2 8.5 %copy.159 = f32[2,16,128,4,64]{2,4,1,3,0:T(8,128)} copy(f32[2,16,128,4,64]{4,3,0,2,1:T(4,128)} %bitcast.311) | data formatting | bytes 8388608 | tf_op jit(solution)/shard_map/all_to_all | solution.py:131
  539.7 5.5 copy.137
  545.3 8.6 %all_to_all.82 = f32[2,128,4,1024]{3,2,0,1:T(4,128)S(1)} all-to-all(f32[2,128,4,1024]{3,2,0,1:T(4,128)} %copy.137), channel_id=1, replica_groups=mesh['trans'=16,'los'=2] {'los'}, dimensions={1} | all-to-all | bytes 8388608 | tf_op jit(solution)/shard_map/all_to_all | solution.py:130
  558.1 2.9 copy.139
  561.1 2.9 reshape_squeeze.14
  564.0 3.3 fusion.204
  567.3 2.9 copy.140
  570.2 3.1 reshape_squeeze.15
  576.7 3.7 convolution_subtract_fusion.1
  584.6 3.4 fusion.135
  588.0 3.8 multiply_bitcast_fusion.1
  591.7 4.8 copy.141
  596.5 5.6 multiply_bitcast_fusion
  602.1 4.8 copy.142
  606.9 7.2 %maximum_bitcast_fusion.1 = f32[2,4,64,2048]{2,3,1,0:T(8,128)} fusion(f32[1,64,4,2048]{1,3,2,0:T(8,128)} %bitcast.328, f32[1,64,4,2048]{1,3,2,0:T(8,128)} %bitcast.324), kind=kLoop, calls=%fused_computation.11 | loop fusion | flops 1048576 | bytes 8388608 | tf_op jit(solution)/shard_map/transpose | solution.py:138
  614.1 6.8 %copy.143 = f32[2,4,64,2048]{3,2,1,0:T(8,128)} copy(f32[2,4,64,2048]{2,3,1,0:T(8,128)} %maximum_bitcast_fusion.1) | data formatting | bytes 8388608 | tf_op jit(solution)/shard_map/transpose | solution.py:138
  (93 shorter events, 46.3 us)
Async XLA Ops:
  8.9 21.8 %copy-start.19 = (s32[2]{0:T(128)S(1)}, s32[2]{0:T(128)}, u32[]{:S(2)}) copy-start(s32[2]{0:T(128)} %param.9) | copy-start | bytes 28
  8.9 23.1 %copy-start.16 = (f32[2,2048]{1,0:T(2,128)S(1)}, f32[2,2048]{1,0:T(2,128)}, u32[]{:S(2)}) copy-start(f32[2,2048]{1,0:T(2,128)} %param.8) | copy-start | bytes 49156
  8.9 23.1 %copy-start.17 = (f32[2,2048]{1,0:T(2,128)S(1)}, f32[2,2048]{1,0:T(2,128)}, u32[]{:S(2)}) copy-start(f32[2,2048]{1,0:T(2,128)} %param.7) | copy-start | bytes 49156
  21.8 23.9 %all-to-all-start = ((bf16[16,2,8192]{2,1,0:T(2,128)(2,1)}), bf16[16,2,8192]{2,1,0:T(2,128)(2,1)S(1)}, u32[]{:S(2)}, u32[]{:S(2)}) async-start(bf16[16,2,8192]{2,1,0:T(2,128)(2,1)} %reshape.416), calls=%async_computation | async-start | bytes 1048576 | tf_op jit(solution)/shard_map/all_to_all | solution.py:73
  69.9 16.6 %copy-start.20 = (s32[2]{0:T(128)S(1)}, s32[2]{0:T(128)}, u32[]{:S(2)}) copy-start(s32[2]{0:T(128)} %param.10) | copy-start | bytes 28
  69.9 17.9 %copy-start.18 = (f32[4,2]{0,1:T(2,128)S(1)}, f32[4,2]{0,1:T(2,128)}, u32[]{:S(2)}) copy-start(f32[4,2]{0,1:T(2,128)} %param.11) | copy-start | bytes 100
  82.4 18.4 %all-to-all-start.1 = ((bf16[16,2,8192]{2,1,0:T(2,128)(2,1)}), bf16[16,2,8192]{2,1,0:T(2,128)(2,1)S(1)}, u32[]{:S(2)}, u32[]{:S(2)}) async-start(bf16[16,2,8192]{2,1,0:T(2,128)(2,1)} %reshape.418), calls=%async_computation.1 | async-start | bytes 1048576 | tf_op jit(solution)/shard_map/all_to_all | solution.py:97
  86.4 80.3 %reduce-scatter.3.cloned.1.call-start = ((), (), s32[]{:S(2)}) async-start(), calls=%async_computation.7 | async-start | bytes 6291456 | tf_op jit(solution)/shard_map/reduce_scatter | solution.py:108
  128.5 6.5 %copy-start.5 = (f32[128,4,16,128]{3,2,1,0:T(8,128)}, f32[128,4,16,128]{3,2,1,0:T(8,128)S(1)}, u32[]{:S(2)}) copy-start(f32[128,4,16,128]{3,2,1,0:T(8,128)S(1)} %get-tuple-element.10) | copy-start | bytes 12582916
  128.5 6.5 %copy-start.3 = (f32[128,4,16,128]{3,2,1,0:T(8,128)}, f32[128,4,16,128]{3,2,1,0:T(8,128)S(1)}, u32[]{:S(2)}) copy-start(f32[128,4,16,128]{3,2,1,0:T(8,128)S(1)} %get-tuple-element.9) | copy-start | bytes 12582916
  146.2 31.0 %reduce-scatter.5.cloned.1.call-start = ((), (), s32[]{:S(2)}) async-start(), calls=%async_computation.8 | async-start | bytes 6291456 | tf_op jit(solution)/shard_map/reduce_scatter | solution.py:109
  146.2 9.5 %copy-start.4 = (f32[128,4,16,128]{3,2,1,0:T(8,128)S(1)}, f32[128,4,16,128]{3,2,1,0:T(8,128)}, u32[]{:S(2)}) copy-start(f32[128,4,16,128]{3,2,1,0:T(8,128)} %copy-done.3) | copy-start | bytes 12582916
  184.6 87.3 %all-to-all-start.2 = ((f32[2,128,4,1024]{1,2,0,3:T(4,128)}), f32[2,128,4,1024]{1,2,0,3:T(4,128)}, u32[]{:S(2)}, u32[]{:S(2)}) async-start(f32[2,128,4,1024]{1,2,0,3:T(4,128)} %copy.123), calls=%async_computation.4 | async-start | bytes 8388608 | tf_op jit(solution)/shard_map/all_to_all | solution.py:111
  284.6 6.0 copy-start.1
  304.1 4.5 copy-start.15
  320.4 3.3 copy-start.6
  327.0 1.3 copy-start.8
  328.3 2.0 copy-start.13
  330.2 3.7 copy-start.7
  336.0 5.6 copy-start.2
  564.0 3.3 copy-start.9
  564.0 3.3 copy-start.14
  573.4 1.3 copy-start.11
  574.7 2.0 copy-start.12
  576.7 3.7 copy-start.10
  582.4 5.6 copy-start
Sparse Core Ops, SparseCore 0:
  146.3 10.2 reduce-scatter.2
  166.8 10.2 reduce-scatter.4
where the time goes:
time: 634 us; the launch traced here: 628 us
  local copies, waits for them, and re-layouts  147 us (23%)
  matrix products  145 us (23%)
  blocking collectives  122 us (19%)
  waiting for transfers between devices  115 us (18%)
  other arithmetic  64.5 us (10%)
  starting transfers between devices  19.9 us (3%)
  between operations  14.4 us (2%)
    all_to_all x1, blocking collectives, body(): lax.all_to_all(returned, 'trans', split_axis=1, concat_axis=3, tiled=True)  114 us
    all_to_all x1, waiting for transfers between devices, body(): lax.all_to_all(jnp.stack([summed_real, summed_imag]), 'trans', split_axis...  78.7 us
    dot_general x16, matrix products, second_pass(): return jnp.einsum('...km,mj->...kj', values, table, precision=highest)  74.2 us
    dot_general x16, matrix products, first_pass(): return jnp.einsum('kn,...nm->...km', table, values, precision=highest)  42.8 us
    unnamed x54, local copies, waits for them, and re-layouts  33.2 us
    unnamed x2, other arithmetic  23.1 us
    mul x4, local copies, waits for them, and re-layouts, fourier(): return (out_real * scale, out_imag * scale)  18.3 us
    transpose x1, local copies, waits for them, and re-layouts, body(): returned = jnp.stack([back_real, back_imag]).transpose(0, 3, 1, 2)  15.3 us
  transfers between devices with their start and end apart: 5, of which 4 were waited for; matrix products, arithmetic and copies ran while one was open for 4% of the time, Pallas kernels for 0%

commit v1 on v0

--- a/solution.py
+++ b/solution.py
@@ -127,12 +127,20 @@
     kernel_imag = first_factor * freq_imag + second_factor * freq_real
     back_real, back_imag = fourier(kernel_real, kernel_imag, True)
     returned = jnp.stack([back_real, back_imag]).transpose(0, 3, 1, 2)
-    rows_local = lax.all_to_all(
-        lax.all_to_all(returned, "trans", split_axis=1, concat_axis=3, tiled=True),
-        "los",
-        split_axis=1,
-        concat_axis=3,
-        tiled=True,
+    rows_local = jnp.concatenate(
+        lax.all_to_all(
+            jnp.stack(
+                jnp.split(
+                    lax.all_to_all(returned, "trans", split_axis=1, concat_axis=3, tiled=True),
+                    lax.axis_size("los"),
+                    axis=1,
+                )
+            ),
+            "los",
+            0,
+            0,
+        ),
+        axis=3,
     )
     final_real, final_imag = fourier(rows_local[0], rows_local[1], True)
     return jnp.stack([final_real, final_imag]).transpose(0, 2, 1, 3)

time: 634 us -> 642 us (1.013)
    another operation x0 -> x2, local copies, waits for them, and re-layouts: none -> 11.6 us  [body(): jnp.stack(jnp.split(lax.all_to_all(returned, 'trans', split_axis=1, conca...]
    all_to_all x3 -> x2, local copies, waits for them, and re-layouts: 14.6 us -> 9.07 us  [body(): lax.all_to_all(returned, 'trans', split_axis=1, concat_axis=3, tiled=True)]
where the time goes in v1:
time: 642 us; the launch traced here: 636 us
  local copies, waits for them, and re-layouts  151 us (24%)
  matrix products  144 us (22%)
  blocking collectives  122 us (19%)
  waiting for transfers between devices  115 us (18%)
  other arithmetic  68.8 us (11%)
  starting transfers between devices  19.6 us (3%)
  between operations  14.6 us (2%)
    all_to_all x1, blocking collectives, body(): lax.all_to_all(returned, 'trans', split_axis=1, concat_axis=3, tiled=True)  114 us
    all_to_all x1, waiting for transfers between devices, body(): lax.all_to_all(jnp.stack([summed_real, summed_imag]), 'trans', split_axis...  78.7 us
    dot_general x16, matrix products, second_pass(): return jnp.einsum('...km,mj->...kj', values, table, precision=highest)  74.1 us
    dot_general x16, matrix products, first_pass(): return jnp.einsum('kn,...nm->...km', table, values, precision=highest)  42.8 us
    unnamed x54, local copies, waits for them, and re-layouts  33.2 us
    unnamed x2, other arithmetic  23.5 us
    mul x4, local copies, waits for them, and re-layouts, fourier(): return (out_real * scale, out_imag * scale)  18.4 us
    transpose x1, local copies, waits for them, and re-layouts, body(): returned = jnp.stack([back_real, back_imag]).transpose(0, 3, 1, 2)  15.3 us
  transfers between devices with their start and end apart: 5, of which 4 were waited for; matrix products, arithmetic and copies ran while one was open for 4% of the time, Pallas kernels for 0%

profile of v1, /device:TPU:0, one launch (start us, length us, event | category | flops | bytes accessed | tf_op | source)
XLA Modules:
  0.0 635.9 jit_solution(4881082690271037705)
XLA Ops:
  9.5 11.5 %reduce = bf16[2048,128]{1,0:T(8,128)(2,1)S(1)} reduce(bf16[2048,1,128]{2,1,0:T(2,128)(2,1)S(1)} %bitcast.335, bf16[]{:T(256)} %broadcast.788), dimensions={1}, to_apply=%bitcast.276.reduce_sub_computation | reduce | bytes 1048578
  21.9 8.6 %all-to-all-start = ((bf16[16,2,8192]{2,1,0:T(2,128)(2,1)}), bf16[16,2,8192]{2,1,0:T(2,128)(2,1)S(1)}, u32[]{:S(2)}, u32[]{:S(2)}) async-start(bf16[16,2,8192]{2,1,0:T(2,128)(2,1)} %reshape.421), calls=%async_computation | async-start | bytes 1048576 | tf_op jit(solution)/shard_map/all_to_all | solution.py:73
  31.9 13.7 %all-to-all-done = bf16[16,2,8192]{2,1,0:T(2,128)(2,1)S(1)} async-done(((bf16[16,2,8192]{2,1,0:T(2,128)(2,1)}), bf16[16,2,8192]{2,1,0:T(2,128)(2,1)S(1)}, u32[]{:S(2)}, u32[]{:S(2)}) %all-to-all-start) | async-done | bytes 524320 | tf_op jit(solution)/shard_map/all_to_all | solution.py:73
  46.4 3.8 fusion.108
  50.2 3.8 fusion.111
  53.9 3.8 fusion.114
  57.7 3.8 fusion.117
  61.5 8.1 %copy.183 = bf16[1,128,2048]{1,0,2:T(2,128)(2,1)S(1)} copy(bf16[1,128,2048]{1,2,0:T(8,128)(2,1)S(1)} %pad_maximum_fusion.2) | data formatting | bytes 1048576 | tf_op jit(solution)/shard_map/concatenate | solution.py:94
  69.7 12.0 %reduce.1 = bf16[2048,128]{1,0:T(8,128)(2,1)S(1)} reduce(bf16[2048,1,128]{2,1,0:T(2,128)(2,1)S(1)} %bitcast.336, bf16[]{:T(256)} %broadcast.788), dimensions={1}, to_apply=%bitcast.302.reduce_sub_computation | reduce | bytes 1048578
  82.6 4.0 all-to-all-start.1
  88.6 12.3 %all-to-all-done.1 = bf16[16,2,8192]{2,1,0:T(2,128)(2,1)S(1)} async-done(((bf16[16,2,8192]{2,1,0:T(2,128)(2,1)}), bf16[16,2,8192]{2,1,0:T(2,128)(2,1)S(1)}, u32[]{:S(2)}, u32[]{:S(2)}) %all-to-all-start.1) | async-done | bytes 524320 | tf_op jit(solution)/shard_map/all_to_all | solution.py:97
  102.2 12.5 %fusion.8 = f32[128,16,128]{2,0,1:T(8,128)S(1)} fusion(bf16[2048,128,1]{0,1,2:T(8,128)(2,1)S(1)} %reshape.405, f32[2048]{0:T(1024)S(1)} %iota_convert_fusion, f32[16,128]{1,0:T(8,128)S(1)} %bitcast.345), kind=kOutput, calls=%fused_computation.13 | convolution fusion | flops 1128267776 | bytes 1589248 | tf_op jit(solution)/shard_map/dot_general | solution.py:99
  115.3 4.1 fusion.12
  119.4 3.9 fusion.10
  125.2 3.2 fusion.36
  128.5 6.5 %fusion.52 = f32[128,4,16,128]{0,3,2,1:T(8,128)S(1)} fusion(f32[128,4,16,128]{3,2,1,0:T(8,128)S(1)} %get-tuple-element.10), kind=kOutput, calls=%fused_computation.78 | convolution fusion | flops 1610858496 | bytes 8388608 | tf_op jit(solution)/shard_map/...km,mj->...kj/dot_general | solution.py:47
  135.0 6.9 %subtract_bitcast_fusion = f32[128,4,128,16]{0,2,3,1:T(8,128)S(1)} fusion(f32[128,4,16,128]{0,3,2,1:T(8,128)S(1)} %fusion.52, f32[128,4,16,128]{3,2,1,0:T(8,128)S(1)} %get-tuple-element.9), kind=kOutput, calls=%fused_computation.59 | convolution fusion | flops 1611890688 | bytes 12582912 | tf_op jit(solution)/shard_map/...km,mj->...kj/dot_general | solution.py:47
  141.9 4.4 copy.119
  146.4 9.2 %fusion.50 = f32[128,4,16,128]{0,3,2,1:T(8,128)S(1)} fusion(f32[128,4,16,128]{3,2,1,0:T(8,128)} %copy-done.5), kind=kOutput, calls=%fused_computation.76 | convolution fusion | flops 1610842112 | bytes 8388608 | tf_op jit(solution)/shard_map/...km,mj->...kj/dot_general | solution.py:47
  155.6 6.5 %add_bitcast_fusion = f32[128,4,128,16]{0,2,3,1:T(8,128)S(1)} fusion(f32[128,4,16,128]{0,3,2,1:T(8,128)S(1)} %fusion.50, f32[128,4,16,128]{3,2,1,0:T(8,128)S(1)} %copy-done.4), kind=kOutput, calls=%fused_computation.58 | convolution fusion | flops 1611907072 | bytes 12582912 | tf_op jit(solution)/shard_map/...km,mj->...kj/dot_general | solution.py:47
  162.1 4.4 copy.124
  166.6 10.4 %reduce-scatter.5.cloned.1.call-done = f32[128,4,1024]{0,2,1:T(8,128)} async-done(((f32[128,4,2048]{0,2,1:T(8,128)}), f32[128,4,1024]{0,2,1:T(8,128)}) %reduce-scatter.5.cloned.1.call-update) | async-done | bytes 2097168 | tf_op jit(solution)/shard_map/reduce_scatter | solution.py:109
  179.6 5.1 copy.125
  184.7 7.0 %all-to-all-start.2 = ((f32[2,128,4,1024]{1,2,0,3:T(4,128)}), f32[2,128,4,1024]{1,2,0,3:T(4,128)}, u32[]{:S(2)}, u32[]{:S(2)}) async-start(f32[2,128,4,1024]{1,2,0,3:T(4,128)} %copy.125), calls=%async_computation.4 | async-start | bytes 8388608 | tf_op jit(solution)/shard_map/all_to_all | solution.py:111
  193.3 78.7 %all-to-all-done.2 = f32[2,128,4,1024]{1,2,0,3:T(4,128)} async-done(((f32[2,128,4,1024]{1,2,0,3:T(4,128)}), f32[2,128,4,1024]{1,2,0,3:T(4,128)}, u32[]{:S(2)}, u32[]{:S(2)}) %all-to-all-start.2) | async-done | bytes 4194336 | tf_op jit(solution)/shard_map/all_to_all | solution.py:111
  272.0 3.0 copy.126
  287.1 3.4 fusion.123
  290.5 3.5 subtract_bitcast_fusion.1
  294.0 4.4 copy.128
  298.4 5.6 add_bitcast_fusion.1
  304.0 4.5 copy.129
  308.5 8.8 %fusion.34 = (f32[4,64,16,128]{1,3,2,0:T(8,128)}, f32[4,64,16,128]{1,3,2,0:T(8,128)}) fusion(f32[64,16,128]{0,2,1:T(8,128)S(1)} %copy-done.15, f32[64,16,128]{0,2,1:T(8,128)S(1)} %get-tuple-element.17, f32[4,64,16,128]{1,3,2,0:T(8,128)} %bitcast.327, f32[4,64,16,128]{1,3,2,0:T(8,128)} %bitcast.325), kind=kLoop, calls=%fused_computation.48 | loop fusion | flops 3145728 | bytes 9437184 | tf_op jit(solution)/shard_map/sub | solution.py:126
  317.3 3.1 copy.130
  320.4 3.3 fusion.208
  323.7 3.3 copy.131
  330.2 3.7 convolution_subtract_fusion.2
  338.1 3.4 fusion.129
  341.5 3.9 multiply_bitcast_fusion.3
  345.5 4.4 copy.134
  349.9 5.6 multiply_bitcast_fusion.2
  355.5 4.4 copy.135
  359.9 4.1 maximum_bitcast_fusion
  364.1 15.3 %copy.182 = f32[2,2048,4,64]{3,2,0,1:T(4,128)} copy(f32[2,2048,4,64]{3,1,2,0:T(8,128)S(1)} %maximum_bitcast_fusion) | data formatting | bytes 8388608 | tf_op jit(solution)/shard_map/transpose | solution.py:129
  379.4 14.6 %reshape.425 = f32[16,1,65536]{2,1,0:T(1,128)} reshape(f32[2048,2,4,64]{3,2,1,0:T(4,128)} %bitcast.315) | data formatting | bytes 8388608
  393.9 113.7 %all_to_all.71 = f32[16,1,65536]{2,1,0:T(1,128)} all-to-all(f32[16,1,65536]{2,1,0:T(1,128)} %reshape.425), channel_id=1, replica_groups=mesh['trans'=16,'los'=2] {'trans'}, dimensions={0} | all-to-all | bytes 8388608 | tf_op jit(solution)/shard_map/all_to_all | solution.py:134
  508.3 13.8 %reduce.2 = f32[16,65536]{1,0:T(8,128)} reduce(f32[16,1,65536]{2,1,0:T(1,128)} %all_to_all.71, f32[]{:T(128)} %broadcast.790), dimensions={1}, to_apply=%all_to_all.61.reduce_sub_computation | reduce | bytes 8388612 | tf_op jit(solution)/shard_map/all_to_all | solution.py:134
  522.1 9.3 %reshape.426 = f32[2048,2,4,64]{3,2,1,0:T(4,128)} reshape(f32[16,65536]{1,0:T(8,128)} %reduce.2) | data formatting | bytes 8388608
  531.4 8.5 %copy.160 = f32[2,16,128,4,64]{2,4,1,3,0:T(8,128)} copy(f32[2,16,128,4,64]{4,3,0,2,1:T(4,128)} %bitcast.314) | data formatting | bytes 8388608 | tf_op jit(solution)/shard_map/all_to_all | solution.py:134
  539.8 4.8 slice_bitcast_fusion.1
  544.7 3.9 pad_maximum_fusion
  548.6 6.8 %copy.139 = f32[2,2,64,4,1024]{4,2,3,1,0:T(8,128)} copy(f32[2,2,64,4,1024]{2,4,3,1,0:T(8,128)} %pad_maximum_fusion) | data formatting | bytes 8388608 | tf_op jit(solution)/shard_map/stack | solution.py:132
  555.3 8.7 %all_to_all.72 = f32[2,2,64,4,1024]{4,2,3,1,0:T(8,128)S(1)} all-to-all(f32[2,2,64,4,1024]{4,2,3,1,0:T(8,128)} %copy.139), channel_id=1, replica_groups=mesh['trans'=16,'los'=2] {'los'}, dimensions={0} | all-to-all | bytes 8388608 | tf_op jit(solution)/shard_map/all_to_all | solution.py:131
  565.8 2.9 copy.140
  571.7 3.2 fusion.204
  574.9 2.9 copy.141
  577.9 3.2 reshape_squeeze.15
  584.4 3.7 convolution_subtract_fusion.1
  592.3 3.4 fusion.135
  595.7 3.8 multiply_bitcast_fusion.1
  599.5 4.8 copy.142
  604.2 5.6 multiply_bitcast_fusion
  609.8 4.8 copy.143
  614.6 7.2 %maximum_bitcast_fusion.1 = f32[2,4,64,2048]{2,3,1,0:T(8,128)} fusion(f32[1,64,4,2048]{1,3,2,0:T(8,128)} %bitcast.330, f32[1,64,4,2048]{1,3,2,0:T(8,128)} %bitcast.326), kind=kLoop, calls=%fused_computation.12 | loop fusion | flops 1048576 | bytes 8388608 | tf_op jit(solution)/shard_map/transpose | solution.py:146
  621.8 6.8 %copy.144 = f32[2,4,64,2048]{3,2,1,0:T(8,128)} copy(f32[2,4,64,2048]{2,3,1,0:T(8,128)} %maximum_bitcast_fusion.1) | data formatting | bytes 8388608 | tf_op jit(solution)/shard_map/transpose | solution.py:146
  (94 shorter events, 49.1 us)
Async XLA Ops:
  8.9 21.6 %copy-start.19 = (s32[2]{0:T(128)S(1)}, s32[2]{0:T(128)}, u32[]{:S(2)}) copy-start(s32[2]{0:T(128)} %param.9) | copy-start | bytes 28
  8.9 22.8 %copy-start.16 = (f32[2,2048]{1,0:T(2,128)S(1)}, f32[2,2048]{1,0:T(2,128)}, u32[]{:S(2)}) copy-start(f32[2,2048]{1,0:T(2,128)} %param.8) | copy-start | bytes 49156
  8.9 22.8 %copy-start.17 = (f32[2,2048]{1,0:T(2,128)S(1)}, f32[2,2048]{1,0:T(2,128)}, u32[]{:S(2)}) copy-start(f32[2,2048]{1,0:T(2,128)} %param.7) | copy-start | bytes 49156
  21.9 23.6 %all-to-all-start = ((bf16[16,2,8192]{2,1,0:T(2,128)(2,1)}), bf16[16,2,8192]{2,1,0:T(2,128)(2,1)S(1)}, u32[]{:S(2)}, u32[]{:S(2)}) async-start(bf16[16,2,8192]{2,1,0:T(2,128)(2,1)} %reshape.421), calls=%async_computation | async-start | bytes 1048576 | tf_op jit(solution)/shard_map/all_to_all | solution.py:73
  69.7 16.9 %copy-start.20 = (s32[2]{0:T(128)S(1)}, s32[2]{0:T(128)}, u32[]{:S(2)}) copy-start(s32[2]{0:T(128)} %param.10) | copy-start | bytes 28
  69.7 18.2 %copy-start.18 = (f32[4,2]{0,1:T(2,128)S(1)}, f32[4,2]{0,1:T(2,128)}, u32[]{:S(2)}) copy-start(f32[4,2]{0,1:T(2,128)} %param.11) | copy-start | bytes 100
  82.6 18.4 %all-to-all-start.1 = ((bf16[16,2,8192]{2,1,0:T(2,128)(2,1)}), bf16[16,2,8192]{2,1,0:T(2,128)(2,1)S(1)}, u32[]{:S(2)}, u32[]{:S(2)}) async-start(bf16[16,2,8192]{2,1,0:T(2,128)(2,1)} %reshape.423), calls=%async_computation.1 | async-start | bytes 1048576 | tf_op jit(solution)/shard_map/all_to_all | solution.py:97
  86.5 80.1 %reduce-scatter.3.cloned.1.call-start = ((), (), s32[]{:S(2)}) async-start(), calls=%async_computation.7 | async-start | bytes 6291456 | tf_op jit(solution)/shard_map/reduce_scatter | solution.py:108
  128.5 6.5 %copy-start.5 = (f32[128,4,16,128]{3,2,1,0:T(8,128)}, f32[128,4,16,128]{3,2,1,0:T(8,128)S(1)}, u32[]{:S(2)}) copy-start(f32[128,4,16,128]{3,2,1,0:T(8,128)S(1)} %get-tuple-element.10) | copy-start | bytes 12582916
  128.5 6.5 %copy-start.3 = (f32[128,4,16,128]{3,2,1,0:T(8,128)}, f32[128,4,16,128]{3,2,1,0:T(8,128)S(1)}, u32[]{:S(2)}) copy-start(f32[128,4,16,128]{3,2,1,0:T(8,128)S(1)} %get-tuple-element.9) | copy-start | bytes 12582916
  146.3 30.7 %reduce-scatter.5.cloned.1.call-start = ((), (), s32[]{:S(2)}) async-start(), calls=%async_computation.8 | async-start | bytes 6291456 | tf_op jit(solution)/shard_map/reduce_scatter | solution.py:109
  146.4 9.2 %copy-start.4 = (f32[128,4,16,128]{3,2,1,0:T(8,128)S(1)}, f32[128,4,16,128]{3,2,1,0:T(8,128)}, u32[]{:S(2)}) copy-start(f32[128,4,16,128]{3,2,1,0:T(8,128)} %copy-done.3) | copy-start | bytes 12582916
  184.7 87.3 %all-to-all-start.2 = ((f32[2,128,4,1024]{1,2,0,3:T(4,128)}), f32[2,128,4,1024]{1,2,0,3:T(4,128)}, u32[]{:S(2)}, u32[]{:S(2)}) async-start(f32[2,128,4,1024]{1,2,0,3:T(4,128)} %copy.125), calls=%async_computation.4 | async-start | bytes 8388608 | tf_op jit(solution)/shard_map/all_to_all | solution.py:111
  284.7 5.8 copy-start.1
  304.0 4.5 copy-start.15
  320.4 3.3 copy-start.6
  326.9 1.3 copy-start.8
  328.3 2.0 copy-start.13
  330.2 3.7 copy-start.7
  335.9 5.6 copy-start.2
  571.7 3.3 copy-start.9
  571.7 3.3 copy-start.14
  581.1 1.3 copy-start.11
  582.4 2.0 copy-start.12
  584.4 3.7 copy-start.10
  590.1 5.6 copy-start
Sparse Core Ops, SparseCore 0:
  146.4 10.2 reduce-scatter.2
  166.7 10.2 reduce-scatter.4
